TPU v7x, 32 devices: a whole 2x2x4 slice. The times are simulated.
32 devices in a mesh: tok: 8 (over y, x, core), blk: 4 (over z).
Axes of the slice: x: 2, y: 2, z: 4, core: 2. Of those that a mesh axis runs over, the one named last changes fastest.
Arguments:
- activations: bfloat16 [4096, 4096], P('tok', 'blk'), may hold values from -52 to 52, as said below
- out_grads: bfloat16 [4096, 4096], P('tok', 'blk'), may hold values from -52 to 52, as said below
Outputs:
- act_inverse: float32 [4096, 4096], P(('tok', 'blk'))
- grad_inverse: float32 [4096, 4096], P(('tok', 'blk'))
Inputs may be any that keep to these rules, and one draw needn't show every extreme that they name: `activations`: real entries. `out_grads`: real entries.
All inputs are finite; a program needn't handle non-finite values.
Results may differ from a plain program's by a relative error of at most 0.02.
Values may be sent and summed in bfloat16 or wider, within the bound.
A program may use at most 64 MiB of HBM per device.

v0:
```python
import jax
import jax.numpy as jnp
from jax import lax
from jax.sharding import PartitionSpec as P

D = 4096
damping = 0.3
epsilon = 1e-06
divisor = 2.0


def column_squares(data):
    values = data.astype(jnp.float32)
    return jnp.sum(values * values, axis=0)


def fold_product(row_block, tile):
    return jnp.dot(
        row_block,
        lax.all_gather(tile, "tok", axis=0, tiled=True),
        preferred_element_type=jnp.float32,
    )


def newton_steps(scaled, identity):
    half = scaled.astype(jnp.bfloat16)
    row_block = lax.all_gather(half, "blk", axis=1, tiled=True)
    square = fold_product(row_block, half)
    cube = fold_product(row_block, square.astype(jnp.bfloat16))
    return 4.0 * identity - 6.0 * scaled + 4.0 * square - cube


def body(activations, out_grads):
    tok_count = lax.axis_size("tok")
    blk_count = lax.axis_size("blk")
    tok_id = lax.axis_index("tok")
    blk_id = lax.axis_index("blk")
    token_count = activations.shape[0] * tok_count
    tile_rows = D // tok_count
    tile_cols = D // blk_count
    full_acts, full_grads = (
        lax.all_gather(activations, "blk", axis=1, tiled=True),
        lax.all_gather(out_grads, "blk", axis=1, tiled=True),
    )
    sums_act, sums_grad = (
        lax.psum(column_squares(full_acts).astype(jnp.bfloat16), "tok").astype(jnp.float32),
        lax.psum(column_squares(full_grads).astype(jnp.bfloat16), "tok").astype(jnp.float32),
    )
    row_ids = tok_id * tile_rows + jnp.arange(tile_rows, dtype=jnp.int32)
    col_ids = blk_id * tile_cols + jnp.arange(tile_cols, dtype=jnp.int32)
    identity = (row_ids[:, None] == col_ids[None, :]).astype(jnp.float32)

    def damped_tile(full, local, sums):
        gram_tile = lax.psum_scatter(
            lax.dot_general(
                full, local, (((0,), (0,)), ((), ())), preferred_element_type=jnp.float32
            ).astype(jnp.bfloat16),
            "tok",
            scatter_dimension=0,
            tiled=True,
        ).astype(jnp.float32)
        inverse = lax.rsqrt(sums / token_count + epsilon)
        inverse_rows = lax.dynamic_slice_in_dim(inverse, tok_id * tile_rows, tile_rows)
        inverse_cols = lax.dynamic_slice_in_dim(inverse, blk_id * tile_cols, tile_cols)
        return (
            gram_tile / token_count * inverse_rows[:, None] * inverse_cols[None, :]
            + damping * identity
        )

    damped_act = damped_tile(full_acts, activations, sums_act)
    damped_grad = damped_tile(full_grads, out_grads, sums_grad)
    results = []
    for damped in (damped_act, damped_grad):
        scaled = damped / divisor
        result_tile = newton_steps(scaled, identity)
        results.append(
            lax.all_to_all(
                result_tile.astype(jnp.bfloat16), "blk", split_axis=0, concat_axis=1, tiled=True
            ).astype(result_tile.dtype)
        )
    return (results[0], results[1])


def solution(mesh):
    placed = (P("tok", "blk"), P("tok", "blk"))
    return jax.shard_map(
        body,
        mesh=mesh,
        in_specs=placed,
        out_specs=(P(("tok", "blk"), None), P(("tok", "blk"), None)),
        check_vma=False,
    )
```

profile of v0, /device:TPU:0, one launch (start us, length us, event | category | flops | bytes accessed | tf_op | source)
XLA Modules:
  0.0 763.5 jit_solution(1316433522095304969)
XLA Ops:
  7.2 0.0 copy-start.1
  7.2 0.0 all-gather.9.cloned.1.call-start
  7.2 0.7 all-gather.9.cloned.1.call-update
  7.9 0.0 all-gather.17.cloned.1.call-start
  8.0 0.7 all-gather.17.cloned.1.call-update
  8.7 0.0 reduce-scatter.3.cloned.1.call-start
  8.7 84.3 %all-gather.9.cloned.1.call-done = bf16[512,4096]{1,0:T(8,128)(2,1)} async-done(((bf16[512,1024]{1,0:T(8,128)(2,1)}), bf16[512,4096]{1,0:T(8,128)(2,1)}) %all-gather.9.cloned.1.call-update) | async-done | bytes 4194320 | tf_op jit(solution)/shard_map/all_gather | solution.py:42
  93.0 0.0 copy-done.1
  93.0 9.1 %convolution_convert_fusion.1 = bf16[4096,1024]{1,0:T(8,128)(2,1)} fusion(bf16[512,4096]{1,0:T(8,128)(2,1)} %all-gather.9.cloned.1.call-done, bf16[512,1024]{1,0:T(8,128)(2,1)S(1)} %copy-done.1), kind=kOutput, calls=%fused_computation.3 | convolution fusion | flops 4299161600 | bytes 13631488 | tf_op jit(solution)/shard_map/dot_general | solution.py:55
  102.1 0.0 copy-start.2
  102.1 0.0 reduce-scatter.3.cloned.1.call-update
  102.2 0.0 reduce-scatter.5.cloned.1.call-start
  102.2 71.7 %all-gather.17.cloned.1.call-done = bf16[512,4096]{1,0:T(8,128)(2,1)} async-done(((bf16[512,1024]{1,0:T(8,128)(2,1)}), bf16[512,4096]{1,0:T(8,128)(2,1)}) %all-gather.17.cloned.1.call-update) | async-done | bytes 4194320 | tf_op jit(solution)/shard_map/all_gather | solution.py:43
  173.9 0.0 copy-done.2
  173.9 9.0 %convolution_convert_fusion = bf16[4096,1024]{1,0:T(8,128)(2,1)} fusion(bf16[512,4096]{1,0:T(8,128)(2,1)} %all-gather.17.cloned.1.call-done, bf16[512,1024]{1,0:T(8,128)(2,1)S(1)} %copy-done.2), kind=kOutput, calls=%fused_computation.2 | convolution fusion | flops 4299161600 | bytes 13631488 | tf_op jit(solution)/shard_map/dot_general | solution.py:55
  182.9 0.0 reduce-scatter.5.cloned.1.call-update
  182.9 0.0 all-gather.19.cloned.1.call-start
  183.0 0.0 copy-start
  183.0 4.2 multiply_reduce_fusion
  187.1 1.0 copy-done
  188.2 0.9 multiply_reduce_fusion.1
  189.1 24.5 %all-reduce = (bf16[4096]{0:T(1024)(128)(2,1)S(1)}, bf16[4096]{0:T(1024)(128)(2,1)S(1)}) all-reduce(bf16[4096]{0:T(1024)(128)(2,1)S(1)} %multiply_reduce_fusion.1, bf16[4096]{0:T(1024)(128)(2,1)S(1)} %multiply_reduce_fusion), channel_id=1, replica_groups=mesh['tok'=8,'blk'=4] {'tok'}, use_global_device_ids=true, to_apply=%region_2.0 | all-reduce | flops 8192 | bytes 32768 | tf_op jit(solution)/shard_map/psum | solution.py:46
  213.6 0.1 dynamic-slice_multiply_fusion
  213.7 0.1 dynamic-slice_multiply_fusion.1
  213.8 33.8 %reduce-scatter.3.cloned.1.call-done = bf16[512,1024]{1,0:T(8,128)(2,1)} async-done(((bf16[4096,1024]{1,0:T(8,128)(2,1)}), bf16[512,1024]{1,0:T(8,128)(2,1)}) %reduce-scatter.3.cloned.1.call-update) | async-done | bytes 1048592 | tf_op jit(solution)/shard_map/reduce_scatter | solution.py:54
  247.6 74.8 %reduce-scatter.5.cloned.1.call-done = bf16[512,1024]{1,0:T(8,128)(2,1)} async-done(((bf16[4096,1024]{1,0:T(8,128)(2,1)}), bf16[512,1024]{1,0:T(8,128)(2,1)}) %reduce-scatter.5.cloned.1.call-update) | async-done | bytes 1048592 | tf_op jit(solution)/shard_map/reduce_scatter | solution.py:54
  322.4 3.8 multiply_convert_fusion
  326.2 0.0 all-gather.19.cloned.1.call-update
  326.2 0.0 all-gather.21.cloned.1.call-start
  326.3 0.5 all-gather.21.cloned.1.call-update
  326.8 0.0 all-gather.11.cloned.1.call-start
  326.9 0.7 all-gather.11.cloned.1.call-update
  327.6 0.0 all-gather.13.cloned.1.call-start
  327.6 0.7 all-gather.13.cloned.1.call-update
  328.3 0.0 all-gather.23.cloned.1.call-start
  328.4 78.8 %all-gather.19.cloned.1.call-done = bf16[512,4096]{1,0:T(8,128)(2,1)} async-done(((bf16[512,1024]{1,0:T(8,128)(2,1)}), bf16[512,4096]{1,0:T(8,128)(2,1)}) %all-gather.19.cloned.1.call-update) | async-done | bytes 4194320 | tf_op jit(solution)/shard_map/all_gather | solution.py:27
  407.1 55.1 %all-gather.21.cloned.1.call-done = bf16[4096,1024]{1,0:T(8,128)(2,1)} async-done(((bf16[512,1024]{1,0:T(8,128)(2,1)}), bf16[4096,1024]{1,0:T(8,128)(2,1)}) %all-gather.21.cloned.1.call-update) | async-done | bytes 8388624 | tf_op jit(solution)/shard_map/all_gather | solution.py:20
  462.2 10.1 %fusion.9 = (bf16[512,1024]{1,0:T(8,128)(2,1)}, f32[512,1024]{1,0:T(8,128)S(1)}) fusion(bf16[512,4096]{1,0:T(8,128)(2,1)} %all-gather.19.cloned.1.call-done, bf16[4096,1024]{1,0:T(8,128)(2,1)} %all-gather.21.cloned.1.call-done), kind=kOutput, calls=%fused_computation.26 | convolution fusion | flops 4295491584 | bytes 15728640 | tf_op jit(solution)/shard_map/dot_general | solution.py:18
  472.4 0.0 all-gather.23.cloned.1.call-update
  472.4 0.0 copy-start.4
  472.4 0.2 all-gather.15.cloned.1.call-start
  472.6 72.5 %all-gather.11.cloned.1.call-done = bf16[512,4096]{1,0:T(8,128)(2,1)} async-done(((bf16[512,1024]{1,0:T(8,128)(2,1)}), bf16[512,4096]{1,0:T(8,128)(2,1)}) %all-gather.11.cloned.1.call-update) | async-done | bytes 4194320 | tf_op jit(solution)/shard_map/all_gather | solution.py:27
  545.1 55.2 %all-gather.13.cloned.1.call-done = bf16[4096,1024]{1,0:T(8,128)(2,1)} async-done(((bf16[512,1024]{1,0:T(8,128)(2,1)}), bf16[4096,1024]{1,0:T(8,128)(2,1)}) %all-gather.13.cloned.1.call-update) | async-done | bytes 8388624 | tf_op jit(solution)/shard_map/all_gather | solution.py:20
  600.4 10.8 %fusion.8 = (bf16[512,1024]{1,0:T(8,128)(2,1)}, f32[512,1024]{1,0:T(8,128)}) fusion(bf16[512,4096]{1,0:T(8,128)(2,1)} %all-gather.11.cloned.1.call-done, bf16[4096,1024]{1,0:T(8,128)(2,1)} %all-gather.13.cloned.1.call-done), kind=kOutput, calls=%fused_computation.25 | convolution fusion | flops 4295491584 | bytes 15728640 | tf_op jit(solution)/shard_map/dot_general | solution.py:18
  611.2 0.0 all-gather.15.cloned.1.call-update
  611.2 45.4 %all-gather.23.cloned.1.call-done = bf16[4096,1024]{1,0:T(8,128)(2,1)} async-done(((bf16[512,1024]{1,0:T(8,128)(2,1)}), bf16[4096,1024]{1,0:T(8,128)(2,1)}) %all-gather.23.cloned.1.call-update) | async-done | bytes 8388624 | tf_op jit(solution)/shard_map/all_gather | solution.py:20
  656.6 0.0 copy-done.4
  656.6 10.6 %fusion.7 = bf16[512,1024]{1,0:T(8,128)(2,1)} fusion(f32[512,1024]{1,0:T(8,128)S(1)} %get-tuple-element.9, bf16[512,1024]{1,0:T(8,128)(2,1)S(1)} %copy-done.4, bf16[512,4096]{1,0:T(8,128)(2,1)} %all-gather.19.cloned.1.call-done, bf16[4096,1024]{1,0:T(8,128)(2,1)} %all-gather.23.cloned.1.call-done, f32[1024]{0:T(1024)S(1)} %dynamic_slice.15, ...), kind=kOutput, calls=%fused_computation.14 | convolution fusion | flops 4301783040 | bytes 16789504 | tf_op jit(solution)/shard_map/dot_general | solution.py:18
  667.2 0.0 copy-start.3
  667.2 4.7 all-to-all-start.1
  671.9 41.2 %all-gather.15.cloned.1.call-done = bf16[4096,1024]{1,0:T(8,128)(2,1)} async-done(((bf16[512,1024]{1,0:T(8,128)(2,1)}), bf16[4096,1024]{1,0:T(8,128)(2,1)}) %all-gather.15.cloned.1.call-update) | async-done | bytes 8388624 | tf_op jit(solution)/shard_map/all_gather | solution.py:20
  713.2 0.0 copy-done.3
  713.2 11.1 %fusion.4 = bf16[512,1024]{1,0:T(8,128)(2,1)} fusion(f32[512,1024]{1,0:T(8,128)} %get-tuple-element.7, bf16[512,1024]{1,0:T(8,128)(2,1)S(1)} %copy-done.3, bf16[512,4096]{1,0:T(8,128)(2,1)} %all-gather.11.cloned.1.call-done, bf16[4096,1024]{1,0:T(8,128)(2,1)} %all-gather.15.cloned.1.call-done, f32[1024]{0:T(1024)S(1)} %dynamic_slice.13, ...), kind=kOutput, calls=%fused_computation.11 | convolution fusion | flops 4301783040 | bytes 16789504 | tf_op jit(solution)/shard_map/dot_general | solution.py:18
  724.3 0.0 all-to-all-done.1
  724.3 4.6 all-to-all-start
  728.9 0.2 convert_bitcast_fusion
  729.1 1.5 copy.7
  730.6 24.4 %all-to-all-done = bf16[4,128,1024]{2,1,0:T(8,128)(2,1)S(1)} async-done(((bf16[4,128,1024]{2,1,0:T(8,128)(2,1)}), bf16[4,128,1024]{2,1,0:T(8,128)(2,1)S(1)}, u32[]{:S(2)}, u32[]{:S(2)}) %all-to-all-start) | async-done | bytes 1048608 | tf_op jit(solution)/shard_map/all_to_all | solution.py:77
  755.0 0.2 convert_bitcast_fusion.1
  755.2 1.5 copy.6
  (5 shorter events, 0.0 us)
Async XLA Ops:
  7.2 85.9 %copy-start.1 = (bf16[512,1024]{1,0:T(8,128)(2,1)S(1)}, bf16[512,1024]{1,0:T(8,128)(2,1)}, u32[]{:S(2)}) copy-start(bf16[512,1024]{1,0:T(8,128)(2,1)} %param.2) | copy-start | bytes 3145732
  7.2 85.9 %all-gather.9.cloned.1.call-start = ((), (), s32[]{:S(2)}) async-start(), calls=%async_computation.4 | async-start | bytes 5242880 | tf_op jit(solution)/shard_map/all_gather | solution.py:42
  7.9 166.0 %all-gather.17.cloned.1.call-start = ((), (), s32[]{:S(2)}) async-start(), calls=%async_computation.9 | async-start | bytes 5242880 | tf_op jit(solution)/shard_map/all_gather | solution.py:43
  8.7 238.9 %reduce-scatter.3.cloned.1.call-start = ((), (), s32[]{:S(2)}) async-start(), calls=%async_computation.5 | async-start | bytes 9437184 | tf_op jit(solution)/shard_map/reduce_scatter | solution.py:54
  102.1 71.7 %copy-start.2 = (bf16[512,1024]{1,0:T(8,128)(2,1)S(1)}, bf16[512,1024]{1,0:T(8,128)(2,1)}, u32[]{:S(2)}) copy-start(bf16[512,1024]{1,0:T(8,128)(2,1)} %param.3) | copy-start | bytes 3145732
  102.2 220.2 %reduce-scatter.5.cloned.1.call-start = ((), (), s32[]{:S(2)}) async-start(), calls=%async_computation.10 | async-start | bytes 9437184 | tf_op jit(solution)/shard_map/reduce_scatter | solution.py:54
  182.9 224.3 %all-gather.19.cloned.1.call-start = ((), (), s32[]{:S(2)}) async-start(), calls=%async_computation.11 | async-start | bytes 5242880 | tf_op jit(solution)/shard_map/all_gather | solution.py:27
  183.0 5.2 copy-start
  326.2 136.0 %all-gather.21.cloned.1.call-start = ((), (), s32[]{:S(2)}) async-start(), calls=%async_computation.12 | async-start | bytes 9437184 | tf_op jit(solution)/shard_map/all_gather | solution.py:20
  326.8 218.3 %all-gather.11.cloned.1.call-start = ((), (), s32[]{:S(2)}) async-start(), calls=%async_computation.6 | async-start | bytes 5242880 | tf_op jit(solution)/shard_map/all_gather | solution.py:27
  327.6 272.8 %all-gather.13.cloned.1.call-start = ((), (), s32[]{:S(2)}) async-start(), calls=%async_computation.7 | async-start | bytes 9437184 | tf_op jit(solution)/shard_map/all_gather | solution.py:20
  328.3 328.3 %all-gather.23.cloned.1.call-start = ((), (), s32[]{:S(2)}) async-start(), calls=%async_computation.13 | async-start | bytes 9437184 | tf_op jit(solution)/shard_map/all_gather | solution.py:20
  472.4 184.2 %copy-start.4 = (bf16[512,1024]{1,0:T(8,128)(2,1)S(1)}, bf16[512,1024]{1,0:T(8,128)(2,1)}, u32[]{:S(2)}) copy-start(bf16[512,1024]{1,0:T(8,128)(2,1)} %reduce-scatter.5.cloned.1.call-done) | copy-start | bytes 3145732
  472.4 240.8 %all-gather.15.cloned.1.call-start = ((), (), s32[]{:S(2)}) async-start(), calls=%async_computation.8 | async-start | bytes 9437184 | tf_op jit(solution)/shard_map/all_gather | solution.py:20
  667.2 46.0 %copy-start.3 = (bf16[512,1024]{1,0:T(8,128)(2,1)S(1)}, bf16[512,1024]{1,0:T(8,128)(2,1)}, u32[]{:S(2)}) copy-start(bf16[512,1024]{1,0:T(8,128)(2,1)} %reduce-scatter.3.cloned.1.call-done) | copy-start | bytes 3145732
  667.2 57.0 %all-to-all-start.1 = ((bf16[4,128,1024]{2,1,0:T(8,128)(2,1)}), bf16[4,128,1024]{2,1,0:T(8,128)(2,1)S(1)}, u32[]{:S(2)}, u32[]{:S(2)}) async-start(bf16[4,128,1024]{2,1,0:T(8,128)(2,1)} %bitcast.2), calls=%async_computation.3 | async-start | bytes 2097152 | tf_op jit(solution)/shard_map/all_to_all | solution.py:77
  724.3 30.7 %all-to-all-start = ((bf16[4,128,1024]{2,1,0:T(8,128)(2,1)}), bf16[4,128,1024]{2,1,0:T(8,128)(2,1)S(1)}, u32[]{:S(2)}, u32[]{:S(2)}) async-start(bf16[4,128,1024]{2,1,0:T(8,128)(2,1)} %bitcast), calls=%async_computation.1 | async-start | bytes 2097152 | tf_op jit(solution)/shard_map/all_to_all | solution.py:77
Sparse Core Ops, SparseCore 0:
  9.6 83.4 all-gather.8
  94.6 79.2 all-gather.16
  177.3 70.1 reduce-scatter.2
  250.9 71.4 reduce-scatter.4
  326.4 80.7 all-gather.18
  409.5 52.7 all-gather.20
  464.4 80.7 all-gather.10
  547.6 52.7 all-gather.12
  602.3 54.2 all-gather.22
  658.9 54.2 all-gather.14
where the time goes:
time: 764 us
  waiting for transfers between devices  641 us (84%)
  matrix products  60.7 us (8%)
  blocking collectives  24.5 us (3%)
  between operations  14.3 us (2%)
  starting transfers between devices  9.9 us (1%)
  other arithmetic  9.53 us (1%)
    all_gather x4, waiting for transfers between devices, fold_product(): lax.all_gather(tile, 'tok', axis=0, tiled=True)  197 us
    all_gather x2, waiting for transfers between devices, newton_steps(): row_block = lax.all_gather(half, 'blk', axis=1, tiled=True)  151 us
    reduce_scatter x2, waiting for transfers between devices, damped_tile(): lax.psum_scatter(lax.dot_general(full, local, (((0,), (0,)), ((), ())), p...  109 us
    all_gather x1, waiting for transfers between devices, body(): lax.all_gather(activations, 'blk', axis=1, tiled=True)  84.3 us
    all_gather x1, waiting for transfers between devices, body(): lax.all_gather(out_grads, 'blk', axis=1, tiled=True)  71.7 us
    dot_general x4, matrix products, fold_product(): jnp.dot(row_block, lax.all_gather(tile, 'tok', axis=0, tiled=True), prefe...  42.6 us
    psum x1, blocking collectives, body(): lax.psum(column_squares(full_acts).astype(jnp.bfloat16), 'tok')  24.5 us
    all_to_all x2, waiting for transfers between devices, body(): lax.all_to_all(result_tile.astype(jnp.bfloat16), 'blk', split_axis=0, con...  24.4 us
  transfers between devices with their start and end apart: 12, of which 11 were waited for; matrix products, arithmetic and copies ran while one was open for 9% of the time, Pallas kernels for 0%

commit v1 on v0

--- a/solution.py
+++ b/solution.py
@@ -1,12 +1,21 @@
+import functools
 import jax
 import jax.numpy as jnp
 from jax import lax
 from jax.sharding import PartitionSpec as P
+from jax.lax import all_gather
 
 D = 4096
 damping = 0.3
 epsilon = 1e-06
 divisor = 2.0
+
+
+def supply_all_the_gates(sample, peer_axis, array_dim):
+    return jnp.concatenate(all_gather(sample, peer_axis), array_dim)
+
+
+state_form = functools.partial(supply_all_the_gates, peer_axis="blk", array_dim=1)
 
 
 def column_squares(data):
@@ -24,7 +33,7 @@
 
 def newton_steps(scaled, identity):
     half = scaled.astype(jnp.bfloat16)
-    row_block = lax.all_gather(half, "blk", axis=1, tiled=True)
+    row_block = state_form(half)
     square = fold_product(row_block, half)
     cube = fold_product(row_block, square.astype(jnp.bfloat16))
     return 4.0 * identity - 6.0 * scaled + 4.0 * square - cube

time: 764 us -> 763 us (level)
  waiting for transfers between devices: 641 us -> 625 us
  local copies, waits for them, and re-layouts: 4 us -> 16.4 us
    all_gather x4, waiting for transfers between devices: 197 us -> 183 us  [fold_product(): lax.all_gather(tile, 'tok', axis=0, tiled=True)]
    all_gather x0 -> x2, local copies, waits for them, and re-layouts: none -> 12.4 us  [supply_all_the_gates(): return jnp.concatenate(all_gather(sample, peer_axis), array_dim)]
  transfers between devices with their start and end apart: 12 -> 12, of which waited for: 11 -> 11; matrix products, arithmetic and copies ran while one was open for 9% -> 11% of each run, Pallas kernels for 0% -> 0%
where the time goes in v1:
time: 763 us; the launch traced here: 762 us
  waiting for transfers between devices  625 us (82%)
  matrix products  62.2 us (8%)
  blocking collectives  24.5 us (3%)
  local copies, waits for them, and re-layouts  16.4 us (2%)
  between operations  14.3 us (2%)
  starting transfers between devices  9.91 us (1%)
  other arithmetic  9.57 us (1%)
    all_gather x4, waiting for transfers between devices, fold_product(): lax.all_gather(tile, 'tok', axis=0, tiled=True)  183 us
    all_gather x2, waiting for transfers between devices, supply_all_the_gates(): return jnp.concatenate(all_gather(sample, peer_axis), array_dim)  150 us
    reduce_scatter x2, waiting for transfers between devices, damped_tile(): lax.psum_scatter(lax.dot_general(full, local, (((0,), (0,)), ((), ())), p...  109 us
    all_gather x1, waiting for transfers between devices, body(): lax.all_gather(activations, 'blk', axis=1, tiled=True)  84.3 us
    all_gather x1, waiting for transfers between devices, body(): lax.all_gather(out_grads, 'blk', axis=1, tiled=True)  71.6 us
    dot_general x4, matrix products, fold_product(): jnp.dot(row_block, lax.all_gather(tile, 'tok', axis=0, tiled=True), prefe...  44.1 us
    psum x1, blocking collectives, body(): lax.psum(column_squares(full_acts).astype(jnp.bfloat16), 'tok')  24.5 us
    all_to_all x2, waiting for transfers between devices, body(): lax.all_to_all(result_tile.astype(jnp.bfloat16), 'blk', split_axis=0, con...  24.4 us
  transfers between devices with their start and end apart: 12, of which 11 were waited for; matrix products, arithmetic and copies ran while one was open for 11% of the time, Pallas kernels for 0%

profile of v1, /device:TPU:0, one launch (start us, length us, event | category | flops | bytes accessed | tf_op | source)
XLA Modules:
  0.0 761.9 jit_solution(6585637910368741289)
XLA Ops:
  7.2 0.0 copy-start.1
  7.2 0.0 all-gather.11.cloned.1.call-start
  7.2 0.7 all-gather.11.cloned.1.call-update
  7.9 0.0 all-gather.17.cloned.1.call-start
  8.0 0.7 all-gather.17.cloned.1.call-update
  8.7 0.0 reduce-scatter.3.cloned.1.call-start
  8.7 84.3 %all-gather.11.cloned.1.call-done = bf16[512,4096]{1,0:T(8,128)(2,1)} async-done(((bf16[512,1024]{1,0:T(8,128)(2,1)}), bf16[512,4096]{1,0:T(8,128)(2,1)}) %all-gather.11.cloned.1.call-update) | async-done | bytes 4194320 | tf_op jit(solution)/shard_map/all_gather | solution.py:51
  93.0 0.0 copy-done.1
  93.0 9.1 %convolution_convert_fusion.1 = bf16[4096,1024]{1,0:T(8,128)(2,1)} fusion(bf16[512,4096]{1,0:T(8,128)(2,1)} %all-gather.11.cloned.1.call-done, bf16[512,1024]{1,0:T(8,128)(2,1)S(1)} %copy-done.1), kind=kOutput, calls=%fused_computation.3 | convolution fusion | flops 4299161600 | bytes 13631488 | tf_op jit(solution)/shard_map/dot_general | solution.py:64
  102.2 0.0 copy-start.2
  102.2 0.0 reduce-scatter.3.cloned.1.call-update
  102.2 0.0 reduce-scatter.5.cloned.1.call-start
  102.2 71.6 %all-gather.17.cloned.1.call-done = bf16[512,4096]{1,0:T(8,128)(2,1)} async-done(((bf16[512,1024]{1,0:T(8,128)(2,1)}), bf16[512,4096]{1,0:T(8,128)(2,1)}) %all-gather.17.cloned.1.call-update) | async-done | bytes 4194320 | tf_op jit(solution)/shard_map/all_gather | solution.py:52
  173.9 0.0 copy-done.2
  173.9 9.0 %convolution_convert_fusion = bf16[4096,1024]{1,0:T(8,128)(2,1)} fusion(bf16[512,4096]{1,0:T(8,128)(2,1)} %all-gather.17.cloned.1.call-done, bf16[512,1024]{1,0:T(8,128)(2,1)S(1)} %copy-done.2), kind=kOutput, calls=%fused_computation.2 | convolution fusion | flops 4299161600 | bytes 13631488 | tf_op jit(solution)/shard_map/dot_general | solution.py:64
  182.9 0.0 reduce-scatter.5.cloned.1.call-update
  182.9 0.0 all-gather.25.cloned.1.call-start
  183.0 0.0 copy-start
  183.0 4.2 multiply_reduce_fusion
  187.1 1.0 copy-done
  188.2 0.9 multiply_reduce_fusion.1
  189.1 24.5 %all-reduce = (bf16[4096]{0:T(1024)(128)(2,1)S(1)}, bf16[4096]{0:T(1024)(128)(2,1)S(1)}) all-reduce(bf16[4096]{0:T(1024)(128)(2,1)S(1)} %multiply_reduce_fusion.1, bf16[4096]{0:T(1024)(128)(2,1)S(1)} %multiply_reduce_fusion), channel_id=1, replica_groups=mesh['tok'=8,'blk'=4] {'tok'}, use_global_device_ids=true, to_apply=%region_2.0 | all-reduce | flops 8192 | bytes 32768 | tf_op jit(solution)/shard_map/psum | solution.py:55
  213.6 0.1 dynamic-slice_multiply_fusion
  213.7 0.1 dynamic-slice_multiply_fusion.1
  213.8 33.8 %reduce-scatter.3.cloned.1.call-done = bf16[512,1024]{1,0:T(8,128)(2,1)} async-done(((bf16[4096,1024]{1,0:T(8,128)(2,1)}), bf16[512,1024]{1,0:T(8,128)(2,1)}) %reduce-scatter.3.cloned.1.call-update) | async-done | bytes 1048592 | tf_op jit(solution)/shard_map/reduce_scatter | solution.py:63
  247.6 74.8 %reduce-scatter.5.cloned.1.call-done = bf16[512,1024]{1,0:T(8,128)(2,1)} async-done(((bf16[4096,1024]{1,0:T(8,128)(2,1)}), bf16[512,1024]{1,0:T(8,128)(2,1)}) %reduce-scatter.5.cloned.1.call-update) | async-done | bytes 1048592 | tf_op jit(solution)/shard_map/reduce_scatter | solution.py:63
  322.4 3.8 multiply_convert_fusion
  326.2 0.0 all-gather.25.cloned.1.call-update
  326.3 0.0 all-gather.19.cloned.1.call-start
  326.3 0.5 all-gather.19.cloned.1.call-update
  326.8 0.0 all-gather.23.cloned.1.call-start
  326.9 0.7 all-gather.23.cloned.1.call-update
  327.6 0.0 all-gather.13.cloned.1.call-start
  327.6 0.7 all-gather.13.cloned.1.call-update
  328.3 0.0 all-gather.21.cloned.1.call-start
  328.4 78.8 %all-gather.25.cloned.1.call-done = bf16[2048,1024]{1,0:T(8,128)(2,1)} async-done(((bf16[512,1024]{1,0:T(8,128)(2,1)}), bf16[2048,1024]{1,0:T(8,128)(2,1)}) %all-gather.25.cloned.1.call-update) | async-done | bytes 4194320 | tf_op jit(solution)/shard_map/all_gather | solution.py:15
  407.2 6.2 copy.8
  413.4 48.9 %all-gather.19.cloned.1.call-done = bf16[4096,1024]{1,0:T(8,128)(2,1)} async-done(((bf16[512,1024]{1,0:T(8,128)(2,1)}), bf16[4096,1024]{1,0:T(8,128)(2,1)}) %all-gather.19.cloned.1.call-update) | async-done | bytes 8388624 | tf_op jit(solution)/shard_map/all_gather | solution.py:29
  462.3 10.9 %fusion.9 = (bf16[512,1024]{1,0:T(8,128)(2,1)}, f32[512,1024]{1,0:T(8,128)}) fusion(bf16[512,4096]{0,1:T(8,128)(2,1)} %bitcast.30, bf16[4096,1024]{1,0:T(8,128)(2,1)} %all-gather.19.cloned.1.call-done), kind=kOutput, calls=%fused_computation.26 | convolution fusion | flops 4295491584 | bytes 15728640 | tf_op jit(solution)/shard_map/dot_general | solution.py:27
  473.1 0.0 all-gather.21.cloned.1.call-update
  473.1 0.2 all-gather.15.cloned.1.call-start
  473.4 71.2 %all-gather.23.cloned.1.call-done = bf16[2048,1024]{1,0:T(8,128)(2,1)} async-done(((bf16[512,1024]{1,0:T(8,128)(2,1)}), bf16[2048,1024]{1,0:T(8,128)(2,1)}) %all-gather.23.cloned.1.call-update) | async-done | bytes 4194320 | tf_op jit(solution)/shard_map/all_gather | solution.py:15
  544.6 6.2 copy.6
  550.8 48.4 %all-gather.13.cloned.1.call-done = bf16[4096,1024]{1,0:T(8,128)(2,1)} async-done(((bf16[512,1024]{1,0:T(8,128)(2,1)}), bf16[4096,1024]{1,0:T(8,128)(2,1)}) %all-gather.13.cloned.1.call-update) | async-done | bytes 8388624 | tf_op jit(solution)/shard_map/all_gather | solution.py:29
  599.3 0.0 copy-start.4
  599.3 10.9 %fusion.8 = (bf16[512,1024]{1,0:T(8,128)(2,1)}, f32[512,1024]{1,0:T(8,128)}) fusion(bf16[512,4096]{0,1:T(8,128)(2,1)} %bitcast.32, bf16[4096,1024]{1,0:T(8,128)(2,1)} %all-gather.13.cloned.1.call-done), kind=kOutput, calls=%fused_computation.25 | convolution fusion | flops 4295491584 | bytes 15728640 | tf_op jit(solution)/shard_map/dot_general | solution.py:27
  610.2 0.0 all-gather.15.cloned.1.call-update
  610.2 45.2 %all-gather.21.cloned.1.call-done = bf16[4096,1024]{1,0:T(8,128)(2,1)} async-done(((bf16[512,1024]{1,0:T(8,128)(2,1)}), bf16[4096,1024]{1,0:T(8,128)(2,1)}) %all-gather.21.cloned.1.call-update) | async-done | bytes 8388624 | tf_op jit(solution)/shard_map/all_gather | solution.py:29
  655.4 0.0 copy-done.4
  655.4 11.1 %fusion.7 = bf16[512,1024]{1,0:T(8,128)(2,1)} fusion(f32[512,1024]{1,0:T(8,128)} %get-tuple-element.9, bf16[512,1024]{1,0:T(8,128)(2,1)S(1)} %copy-done.4, bf16[512,4096]{0,1:T(8,128)(2,1)} %bitcast.31, bf16[4096,1024]{1,0:T(8,128)(2,1)} %all-gather.21.cloned.1.call-done, f32[1024]{0:T(1024)S(1)} %dynamic_slice.15, f32[512]{0:T(512)S(1)} %dynamic-slice_multiply_fusion, ...), kind=kOutput, calls=%fused_computation.14 | convolution fusion | flops 4301783040 | bytes 16789504 | tf_op jit(solution)/shard_map/dot_general | solution.py:27
  666.6 0.0 copy-start.3
  666.6 4.7 all-to-all-start.1
  671.3 40.1 %all-gather.15.cloned.1.call-done = bf16[4096,1024]{1,0:T(8,128)(2,1)} async-done(((bf16[512,1024]{1,0:T(8,128)(2,1)}), bf16[4096,1024]{1,0:T(8,128)(2,1)}) %all-gather.15.cloned.1.call-update) | async-done | bytes 8388624 | tf_op jit(solution)/shard_map/all_gather | solution.py:29
  711.5 0.0 copy-done.3
  711.5 11.2 %fusion.4 = bf16[512,1024]{1,0:T(8,128)(2,1)} fusion(f32[512,1024]{1,0:T(8,128)} %get-tuple-element.7, bf16[512,1024]{1,0:T(8,128)(2,1)S(1)} %copy-done.3, bf16[512,4096]{0,1:T(8,128)(2,1)} %bitcast.33, bf16[4096,1024]{1,0:T(8,128)(2,1)} %all-gather.15.cloned.1.call-done, f32[1024]{0:T(1024)S(1)} %dynamic_slice.13, ...), kind=kOutput, calls=%fused_computation.11 | convolution fusion | flops 4301783040 | bytes 16789504 | tf_op jit(solution)/shard_map/dot_general | solution.py:27
  722.6 0.0 all-to-all-done.1
  722.6 4.6 all-to-all-start
  727.2 0.2 convert_bitcast_fusion
  727.5 1.5 copy.11
  728.9 24.4 %all-to-all-done = bf16[4,128,1024]{2,1,0:T(8,128)(2,1)S(1)} async-done(((bf16[4,128,1024]{2,1,0:T(8,128)(2,1)}), bf16[4,128,1024]{2,1,0:T(8,128)(2,1)S(1)}, u32[]{:S(2)}, u32[]{:S(2)}) %all-to-all-start) | async-done | bytes 1048608 | tf_op jit(solution)/shard_map/all_to_all | solution.py:86
  753.4 0.2 convert_bitcast_fusion.1
  753.6 1.5 copy.10
  (5 shorter events, 0.0 us)
Async XLA Ops:
  7.2 85.9 %copy-start.1 = (bf16[512,1024]{1,0:T(8,128)(2,1)S(1)}, bf16[512,1024]{1,0:T(8,128)(2,1)}, u32[]{:S(2)}) copy-start(bf16[512,1024]{1,0:T(8,128)(2,1)} %param.2) | copy-start | bytes 3145732
  7.2 85.9 %all-gather.11.cloned.1.call-start = ((), (), s32[]{:S(2)}) async-start(), calls=%async_computation.4 | async-start | bytes 5242880 | tf_op jit(solution)/shard_map/all_gather | solution.py:51
  7.9 166.0 %all-gather.17.cloned.1.call-start = ((), (), s32[]{:S(2)}) async-start(), calls=%async_computation.8 | async-start | bytes 5242880 | tf_op jit(solution)/shard_map/all_gather | solution.py:52
  8.7 238.9 %reduce-scatter.3.cloned.1.call-start = ((), (), s32[]{:S(2)}) async-start(), calls=%async_computation.5 | async-start | bytes 9437184 | tf_op jit(solution)/shard_map/reduce_scatter | solution.py:63
  102.2 71.7 %copy-start.2 = (bf16[512,1024]{1,0:T(8,128)(2,1)S(1)}, bf16[512,1024]{1,0:T(8,128)(2,1)}, u32[]{:S(2)}) copy-start(bf16[512,1024]{1,0:T(8,128)(2,1)} %param.3) | copy-start | bytes 3145732
  102.2 220.2 %reduce-scatter.5.cloned.1.call-start = ((), (), s32[]{:S(2)}) async-start(), calls=%async_computation.9 | async-start | bytes 9437184 | tf_op jit(solution)/shard_map/reduce_scatter | solution.py:63
  182.9 224.3 %all-gather.25.cloned.1.call-start = ((), (), s32[]{:S(2)}) async-start(), calls=%async_computation.13 | async-start | bytes 5242880 | tf_op jit(solution)/shard_map/all_gather | solution.py:15
  183.0 5.2 copy-start
  326.3 136.0 %all-gather.19.cloned.1.call-start = ((), (), s32[]{:S(2)}) async-start(), calls=%async_computation.10 | async-start | bytes 9437184 | tf_op jit(solution)/shard_map/all_gather | solution.py:29
  326.8 217.8 %all-gather.23.cloned.1.call-start = ((), (), s32[]{:S(2)}) async-start(), calls=%async_computation.12 | async-start | bytes 5242880 | tf_op jit(solution)/shard_map/all_gather | solution.py:15
  327.6 271.7 %all-gather.13.cloned.1.call-start = ((), (), s32[]{:S(2)}) async-start(), calls=%async_computation.6 | async-start | bytes 9437184 | tf_op jit(solution)/shard_map/all_gather | solution.py:29
  328.3 327.1 %all-gather.21.cloned.1.call-start = ((), (), s32[]{:S(2)}) async-start(), calls=%async_computation.11 | async-start | bytes 9437184 | tf_op jit(solution)/shard_map/all_gather | solution.py:29
  473.1 238.3 %all-gather.15.cloned.1.call-start = ((), (), s32[]{:S(2)}) async-start(), calls=%async_computation.7 | async-start | bytes 9437184 | tf_op jit(solution)/shard_map/all_gather | solution.py:29
  599.3 56.2 %copy-start.4 = (bf16[512,1024]{1,0:T(8,128)(2,1)S(1)}, bf16[512,1024]{1,0:T(8,128)(2,1)}, u32[]{:S(2)}) copy-start(bf16[512,1024]{1,0:T(8,128)(2,1)} %reduce-scatter.5.cloned.1.call-done) | copy-start | bytes 3145732
  666.6 44.9 %copy-start.3 = (bf16[512,1024]{1,0:T(8,128)(2,1)S(1)}, bf16[512,1024]{1,0:T(8,128)(2,1)}, u32[]{:S(2)}) copy-start(bf16[512,1024]{1,0:T(8,128)(2,1)} %reduce-scatter.3.cloned.1.call-done) | copy-start | bytes 3145732
  666.6 56.0 %all-to-all-start.1 = ((bf16[4,128,1024]{2,1,0:T(8,128)(2,1)}), bf16[4,128,1024]{2,1,0:T(8,128)(2,1)S(1)}, u32[]{:S(2)}, u32[]{:S(2)}) async-start(bf16[4,128,1024]{2,1,0:T(8,128)(2,1)} %bitcast.10), calls=%async_computation.3 | async-start | bytes 2097152 | tf_op jit(solution)/shard_map/all_to_all | solution.py:86
  722.6 30.7 %all-to-all-start = ((bf16[4,128,1024]{2,1,0:T(8,128)(2,1)}), bf16[4,128,1024]{2,1,0:T(8,128)(2,1)S(1)}, u32[]{:S(2)}, u32[]{:S(2)}) async-start(bf16[4,128,1024]{2,1,0:T(8,128)(2,1)} %bitcast.4), calls=%async_computation.1 | async-start | bytes 2097152 | tf_op jit(solution)/shard_map/all_to_all | solution.py:86
Sparse Core Ops, SparseCore 0:
  9.6 83.4 all-gather.10
  94.6 79.2 all-gather.16
  177.3 70.1 reduce-scatter.2
  250.9 71.4 reduce-scatter.4
  326.4 80.7 all-gather.24
  409.5 52.7 all-gather.18
  463.8 80.7 all-gather.22
  546.5 52.7 all-gather.12
  601.2 54.2 all-gather.20
  657.2 54.2 all-gather.14
